TPU v7x, 32 devices: a whole 2x2x4 slice. The times are simulated.
32 devices in a mesh: section: 4 (over z), seq: 4 (over y, x), head: 2 (over core).
Axes of the slice: x: 2, y: 2, z: 4, core: 2. Of those that a mesh axis runs over, the one named last changes fastest.
Arguments:
- text_hidden: bfloat16 [4096, 4096], P('seq'), may hold values from -600 to 600
- norm_gain: float32 [4096], replicated, may hold values from 0.1 to 1.9
- image_features: bfloat16 [8192, 1024], P('seq'), may hold values from -6 to 6
- query_weight: bfloat16 [4096, 4096], P(None, ('section', 'head')), may hold values from -30 to 30
- key_weight: bfloat16 [1024, 1024], P(None, ('section', 'head')), may hold values from -0.75 to 0.75
- value_weight: bfloat16 [1024, 1024], P(None, ('section', 'head')), may hold values from -0.1875 to 0.1875
- output_weight: bfloat16 [4096, 4096], P(('section', 'head')), may hold values from -0.125 to 0.125
- selected: int32 [32, 16], P('seq'), may hold values from 0 to 127, as said below
Outputs:
- attn_output: bfloat16 [4096, 4096], P('seq', ('section', 'head'))
Inputs may be any that keep to these rules, and one draw needn't show every extreme that they name: `selected`: each row names 16 different image blocks. The tiles of one seq index together select at most 32 different blocks from the 32 blocks of any one seq index, and exactly 32 from some seq index.
All inputs are finite; a program needn't handle non-finite values.
Results may differ from a plain program's by a relative error of at most 0.0069.
The roundings to bfloat16 on the way count: a program that leaves them out, or rounds other values in their place, can miss the bound.
Values may be sent and summed in bfloat16 or wider, within the bound.
A program may use at most 128 MiB of HBM per device.

v0:
```python
import functools

import jax
import jax.numpy as jnp
from jax import lax
from jax.experimental import pallas as pl
from jax.experimental.pallas import tpu as pltpu
from jax.sharding import PartitionSpec as P

HEAD_DIM = 128
TILE = 128
BLOCK = 64
EPSILON = 1e-05
CHUNKS = 4
PART_LAG = 4
OUT_LAG = 2
MESH = pl.DeviceIdType.MESH


def kernel(
    sizes,
    text_hbm,
    gain_ref,
    image_hbm,
    wq_hbm,
    wk_hbm,
    wv_hbm,
    wo_hbm,
    sel_ref,
    out_ref,
    text,
    image,
    wq,
    wkv,
    wo_all,
    part_out,
    part_in,
    k_all,
    v_all,
    q_all,
    k_sel,
    v_sel,
    att,
    text_sem,
    image_sem,
    weight_sem,
    kv_send,
    kv_recv,
    fwd_send,
    fwd_recv,
    wo_local,
    wo_send,
    wo_recv,
    z_send,
    z_recv,
    g_send,
    g_recv,
    gf_send,
    gf_recv,
    go_sem,
    a_send,
    a_core,
    r_pair,
    r_core,
    p_send,
    p_recv,
):
    n_sec, n_seq, n_head = sizes
    sec = lax.axis_index("section")
    seq = lax.axis_index("seq")
    head = lax.axis_index("head")
    tiles = q_all.shape[0]
    qk_rows = q_all.shape[1]
    heads = qk_rows // TILE
    width = k_all.shape[-1]
    local_kv = width // HEAD_DIM
    group = heads // local_kv
    topk = sel_ref.shape[1]
    rows_img = image.shape[0]
    blocks_dev = rows_img // BLOCK
    chunk_blocks = blocks_dev // CHUNKS
    chunk_rows = chunk_blocks * BLOCK
    out_cols = out_ref.shape[1]
    text_step = text_sem.shape[0]
    text_rows = text.shape[0] // text_step

    other = 1 - head
    buddy = lax.rem(sec + n_sec // 2, n_sec)
    far = sec + 1 - 2 * lax.rem(sec, 2)
    buddy_far = buddy + 1 - 2 * lax.rem(buddy, 2)
    first = head == 0

    def at(s, h):
        return {"section": s, "seq": seq, "head": h}

    def at_seq(q):
        return {"section": sec, "seq": q, "head": head}

    def remote(src, dst, send, recv, device):
        return pltpu.make_async_remote_copy(
            src_ref=src, dst_ref=dst, send_sem=send, recv_sem=recv, device_id=device, device_id_type=MESH
        )

    weight_loads = [
        pltpu.make_async_copy(wk_hbm, wkv.at[:, pl.ds(0, width)], weight_sem.at[0]),
        pltpu.make_async_copy(wv_hbm, wkv.at[:, pl.ds(width, width)], weight_sem.at[1]),
        pltpu.make_async_copy(wq_hbm, wq, weight_sem.at[2]),
    ]
    image_loads = [
        pltpu.make_async_copy(
            image_hbm.at[pl.ds(c * chunk_rows, chunk_rows)],
            image.at[pl.ds(c * chunk_rows, chunk_rows)],
            image_sem.at[c],
        )
        for c in range(CHUNKS)
    ]
    text_loads = [
        pltpu.make_async_copy(
            text_hbm.at[pl.ds(c * text_rows, text_rows)],
            text.at[pl.ds(c * text_rows, text_rows)],
            text_sem.at[c],
        )
        for c in range(text_step)
    ]
    weight_loads[0].start()
    weight_loads[1].start()
    for load in image_loads:
        load.start()
    weight_loads[2].start()
    for load in text_loads:
        load.start()

    barrier = pltpu.get_barrier_semaphore()
    for d in range(1, n_seq):
        pl.semaphore_signal(barrier, inc=1, device_id=at_seq(lax.rem(seq + d, n_seq)), device_id_type=MESH)
    for d in range(n_sec):
        for e in range(n_head):
            if d or e:
                pl.semaphore_signal(
                    barrier,
                    inc=1,
                    device_id=at(lax.rem(sec + d, n_sec), lax.rem(head + e, n_head)),
                    device_id_type=MESH,
                )
    pl.semaphore_wait(barrier, n_seq - 1 + n_sec * n_head - 1)

    def slot(flag, h):
        return flag * n_head + h

    def wo_cols(s, h):
        return pl.ds(pl.multiple_of((s * n_head + h) * out_cols, out_cols), out_cols)

    wo_own = [
        pltpu.make_async_copy(
            wo_hbm.at[:, wo_cols((sec, far)[side], head)], wo_all.at[side, slot(0, head)], wo_local.at[side]
        )
        for side in range(2)
    ]
    wo_near = [
        remote(
            wo_hbm.at[:, wo_cols((sec, far)[side], other)],
            wo_all.at[side, slot(0, head)],
            wo_send.at[side],
            wo_recv.at[side],
            at(sec, other),
        )
        for side in (1, 0)
    ]
    piece_rows = wo_hbm.shape[0] // n_seq

    def piece_at(side, h, owner):
        return wo_all.at[side, slot(1, h), pl.ds(pl.multiple_of(owner * piece_rows, piece_rows), piece_rows)]

    wo_far = [
        remote(
            wo_hbm.at[
                pl.ds(pl.multiple_of(seq * piece_rows, piece_rows), piece_rows), wo_cols((buddy, buddy_far)[side], h)
            ],
            piece_at(side, head, seq),
            z_send.at[side, i],
            z_recv.at[side, i],
            at(buddy, h),
        )
        for side in (1, 0)
        for i, h in enumerate((head, other))
    ]
    for copy in wo_far + wo_own + wo_near:
        copy.start()

    weight_loads[0].wait()
    weight_loads[1].wait()

    def chunk_at(ref, owner, c):
        return ref.at[pl.ds(owner * blocks_dev + c * chunk_blocks, chunk_blocks)]

    ring = n_seq == 4
    if ring:
        sx, sy = lax.rem(seq, 2), seq // 2
        beside = sy * 2 + (1 - sx)
        across = (1 - sy) * 2 + sx
        peers = [beside, across]
    else:
        peers = [lax.rem(seq + d, n_seq) for d in range(1, n_seq)]

    def kv_copy(kind, peer_at, c):
        ref = (k_all, v_all)[kind]
        return remote(
            chunk_at(ref, seq, c),
            chunk_at(ref, seq, c),
            kv_send.at[kind, peer_at, c],
            kv_recv.at[kind, peer_at, c],
            at_seq(peers[peer_at]),
        )

    def kv_start_early(c):
        if ring:
            kv_copy(0, 1, c).start()
            kv_copy(1, 0, c).start()
        else:
            for p in range(len(peers)):
                kv_copy(0, p, c).start()
                kv_copy(1, p, c).start()

    def kv_start_late():
        if ring:
            for c in range(CHUNKS):
                kv_copy(1, 1, c).start()
                kv_copy(0, 0, c).start()

    for c in range(CHUNKS):
        image_loads[c].wait()
        both = jnp.dot(
            image[c * chunk_rows : (c + 1) * chunk_rows, :], wkv[...], preferred_element_type=jnp.float32
        ).astype(jnp.bfloat16)
        base = pl.ds(seq * blocks_dev + c * chunk_blocks, chunk_blocks)
        k_all[base] = both[:, :width].reshape(chunk_blocks, BLOCK, width)
        v_all[base] = both[:, width:].reshape(chunk_blocks, BLOCK, width)

        @pl.when(first)
        def _():
            kv_start_early(c)

    @pl.when(first)
    def _():
        kv_start_late()

    weight_loads[2].wait()
    for load in text_loads:
        load.wait()

    def query_step(i, carry):
        part = pl.ds(pl.multiple_of(i * text_rows, text_rows), text_rows)
        as_float = text[part, :].astype(jnp.float32)
        inverse = lax.rsqrt(jnp.mean(as_float * as_float, axis=-1, keepdims=True) + EPSILON)
        normed = (as_float * inverse * gain_ref[...]).astype(jnp.bfloat16)
        queries = jnp.dot(normed, wq[...], preferred_element_type=jnp.float32).astype(jnp.bfloat16)
        for u in range(text_rows // TILE):
            for h in range(heads):
                q_all[i * (text_rows // TILE) + u, h * TILE : (h + 1) * TILE, :] = queries[
                    u * TILE : (u + 1) * TILE, h * HEAD_DIM : (h + 1) * HEAD_DIM
                ]
        return carry

    lax.fori_loop(0, text_step, query_step, 0)

    def kv_arrival(kind, peer_at, c):
        ref = (k_all, v_all)[kind]
        back = peer_at if ring else len(peers) - 1 - peer_at
        there = chunk_at(ref, peers[back], c)
        return remote(there, there, kv_send.at[kind, peer_at, c], kv_recv.at[kind, peer_at, c], at_seq(peers[peer_at]))

    def kv_forward(kind, c):
        ref = (k_all, v_all)[kind]
        came, goes = ((across, beside), (beside, across))[kind]
        there = chunk_at(ref, came, c)
        return remote(there, there, fwd_send.at[kind, c], fwd_recv.at[kind, c], at_seq(goes))

    def kv_forwarded(kind, c):
        ref = (k_all, v_all)[kind]
        there = chunk_at(ref, 3 - seq, c)
        return remote(there, there, fwd_send.at[kind, c], fwd_recv.at[kind, c], at_seq(seq))

    @pl.when(jnp.logical_not(first))
    def _():
        pl.semaphore_wait(go_sem, 1)
        for c in range(CHUNKS):
            kv_start_early(c)
        kv_start_late()

    def kv_done(c):
        if ring:
            kv_arrival(0, 0, c).wait_recv()
            kv_arrival(1, 1, c).wait_recv()
            kv_forwarded(0, c).wait_recv()
            kv_forwarded(1, c).wait_recv()
        else:
            for p in range(len(peers)):
                kv_arrival(0, p, c).wait_recv()
                kv_arrival(1, p, c).wait_recv()

    def g_copy(side, i, peer_at):
        piece = piece_at(side, (head, other)[i], seq)
        return remote(piece, piece, g_send.at[side, i, peer_at], g_recv.at[side, i, peer_at], at_seq(peers[peer_at]))

    def g_arrival(side, i, peer_at):
        back = peer_at if ring else len(peers) - 1 - peer_at
        there = piece_at(side, (head, other)[i], peers[back])
        return remote(there, there, g_send.at[side, i, peer_at], g_recv.at[side, i, peer_at], at_seq(peers[peer_at]))

    def g_forward(side, i):
        came, goes = ((across, beside), (beside, across))[i]
        there = piece_at(side, (head, other)[i], came)
        return remote(there, there, gf_send.at[side, i], gf_recv.at[side, i], at_seq(goes))

    def g_forwarded(side, i):
        there = piece_at(side, (head, other)[i], 3 - seq)
        return remote(there, there, gf_send.at[side, i], gf_recv.at[side, i], at_seq(peers[0]))

    def spread_wo(side):
        for i in range(2):
            there = piece_at(side, (head, other)[i], seq)
            remote(there, there, z_send.at[side, i], z_recv.at[side, i], at(buddy, head)).wait_recv()
        for i in range(2):
            if ring:
                g_copy(side, i, 1 - i).start()
            else:
                for p in range(len(peers)):
                    g_copy(side, i, p).start()
        if ring:
            for i in range(2):
                g_copy(side, i, i).start()

    def forward_wo(side):
        if ring:
            for i in range(2):
                g_arrival(side, i, 1 - i).wait_recv()
                g_forward(side, i).start()

    def wo_arrived(side):
        wo_own[side].wait()
        there = wo_all.at[side, slot(0, other)]
        remote(there, there, wo_send.at[side], wo_recv.at[side], at(sec, other)).wait_recv()
        for i in range(2):
            if ring:
                g_arrival(side, i, i).wait_recv()
                g_forwarded(side, i).wait_recv()
            else:
                for p in range(len(peers)):
                    g_arrival(side, i, p).wait_recv()

    if ring:
        for c in range(CHUNKS):
            kv_arrival(0, 1, c).wait_recv()
            kv_forward(0, c).start()
            kv_arrival(1, 0, c).wait_recv()
            kv_forward(1, c).start()

    @pl.when(jnp.logical_not(first))
    def _():
        spread_wo(1)
        spread_wo(0)

    for c in range(CHUNKS - 1):
        kv_done(c)

    @pl.when(first)
    def _():
        pl.semaphore_signal(go_sem, inc=1, device_id=at(sec, other), device_id_type=MESH)

    kv_done(CHUNKS - 1)

    def own_copies(t):
        tile = att.at[slot(0, head), t]
        return (
            remote(tile, att.at[slot(1, head), t], a_send.at[0, t], r_pair.at[t], at(buddy, head)),
            remote(tile, tile, a_send.at[1, t], r_core.at[0, t], at(sec, other)),
        )

    def pair_forward(t):
        tile = att.at[slot(1, head), t]
        return remote(tile, tile, a_core.at[t], r_core.at[1, t], at(sec, other))

    def part_copy(t):
        return remote(part_out.at[t], part_in.at[t], p_send.at[t], p_recv.at[t], at(far, head))

    def attend(t):
        for j in range(topk):
            block = sel_ref[t, j]
            k_sel[j * BLOCK : (j + 1) * BLOCK, :] = k_all[block]
            v_sel[j * BLOCK : (j + 1) * BLOCK, :] = v_all[block]
        for h in range(heads):
            kv = (h // group) * HEAD_DIM
            scores = lax.dot_general(
                q_all[t, h * TILE : (h + 1) * TILE, :],
                k_sel[:, kv : kv + HEAD_DIM],
                (((1,), (1,)), ((), ())),
                preferred_element_type=jnp.float32,
            ) * HEAD_DIM ** (-0.5)
            exponent = jnp.exp(scores - jnp.max(scores, axis=-1, keepdims=True))
            weights = (exponent * (1.0 / jnp.sum(exponent, axis=-1, keepdims=True))).astype(jnp.bfloat16)
            att[slot(0, head), t, :, h * HEAD_DIM : (h + 1) * HEAD_DIM] = jnp.dot(
                weights, v_sel[:, kv : kv + HEAD_DIM], preferred_element_type=jnp.float32
            ).astype(jnp.bfloat16)

    def product(side, t):
        total = None
        for i in range(2 * n_head):
            term = jnp.dot(att[i, t], wo_all[side, i], preferred_element_type=jnp.float32)
            total = term if total is None else total + term
        return total

    lag_part = jnp.where(first, tiles + 1, PART_LAG)
    lag_out = jnp.where(first, tiles + 1 + OUT_LAG, tiles + OUT_LAG)
    at_spread = tiles - 1
    at_forward = jnp.where(first, tiles, PART_LAG - 1)

    def step(s, carry):
        @pl.when(s < tiles)
        def _():
            attend(s)
            for copy in own_copies(s):
                copy.start()

        @pl.when((s >= 1) & (s < tiles + 1))
        def _():
            t = s - 1
            there = att.at[slot(1, head), t]
            remote(there, there, a_send.at[0, t], r_pair.at[t], at(buddy, head)).wait_recv()
            pair_forward(t).start()

        @pl.when(first & (s == at_spread))
        def _():
            spread_wo(1)
            spread_wo(0)

        @pl.when(s == at_forward)
        def _():
            forward_wo(1)

        @pl.when(s == at_forward + 1)
        def _():
            wo_arrived(1)
            forward_wo(0)

        @pl.when((s >= lag_part) & (s < tiles + lag_part))
        def _():
            t = s - lag_part
            for flag in range(2):
                there = att.at[slot(flag, other), t]
                remote(there, there, a_send.at[1, t], r_core.at[flag, t], at(sec, other)).wait_recv()
            part_out[t] = product(1, t).astype(jnp.bfloat16)
            part_copy(t).start()

        @pl.when(s == lag_out)
        def _():
            wo_arrived(0)

        @pl.when((s >= lag_out) & (s < tiles + lag_out))
        def _():
            t = s - lag_out
            own = product(0, t)
            part_copy(t).wait_recv()
            out_ref[pl.ds(pl.multiple_of(t * TILE, TILE), TILE), :] = (own + part_in[t].astype(jnp.float32)).astype(
                out_ref.dtype
            )

        return carry

    lax.fori_loop(0, 2 * tiles + 1 + OUT_LAG, step, 0)

    for copy in wo_near + wo_far:
        copy.wait_send()
    for side in range(2):
        for i in range(2):
            for p in range(len(peers)):
                g_copy(side, i, p).wait_send()
            if ring:
                g_forward(side, i).wait_send()
    for c in range(CHUNKS):
        for kind in range(2):
            for p in range(len(peers)):
                kv_copy(kind, p, c).wait_send()
            if ring:
                kv_forward(kind, c).wait_send()

    def drain(t, carry):
        for copy in own_copies(t) + (pair_forward(t), part_copy(t)):
            copy.wait_send()
        return carry

    lax.fori_loop(0, tiles, drain, 0)


def solution(mesh):
    n_sec, n_seq, n_head = mesh.shape["section"], mesh.shape["seq"], mesh.shape["head"]

    def shards(text, gain, image, wq, wk, wv, wo, selected):
        rows, depth = text.shape
        tiles = rows // TILE
        cols_q = wq.shape[1]
        width = wk.shape[1]
        group = n_sec * n_head
        out_cols = wo.shape[1] // group
        blocks = image.shape[0] // BLOCK * n_seq
        keys = selected.shape[1] * BLOCK
        text_step = max(1, rows // (2 * TILE))
        peers = 2 if n_seq == 4 else n_seq - 1
        bf16 = jnp.bfloat16
        dma = pltpu.SemaphoreType.DMA
        hbm = pl.BlockSpec(memory_space=pl.ANY)
        vmem = pl.BlockSpec(memory_space=pltpu.VMEM)
        return pl.pallas_call(
            functools.partial(kernel, (n_sec, n_seq, n_head)),
            out_shape=jax.ShapeDtypeStruct((rows, out_cols), bf16),
            in_specs=[hbm, vmem, hbm, hbm, hbm, hbm, hbm, pl.BlockSpec(memory_space=pltpu.SMEM)],
            out_specs=vmem,
            scratch_shapes=[
                pltpu.VMEM(text.shape, bf16),
                pltpu.VMEM(image.shape, bf16),
                pltpu.VMEM(wq.shape, bf16),
                pltpu.VMEM((wk.shape[0], 2 * width), bf16),
                pltpu.VMEM((2, 2 * n_head, wo.shape[0], out_cols), bf16),
                pltpu.VMEM((tiles, TILE, out_cols), bf16),
                pltpu.VMEM((tiles, TILE, out_cols), bf16),
                pltpu.VMEM((blocks, BLOCK, width), bf16),
                pltpu.VMEM((blocks, BLOCK, width), bf16),
                pltpu.VMEM((tiles, cols_q // HEAD_DIM * TILE, HEAD_DIM), bf16),
                pltpu.VMEM((keys, width), bf16),
                pltpu.VMEM((keys, width), bf16),
                pltpu.VMEM((2 * n_head, tiles, TILE, cols_q), bf16),
                dma((text_step,)),
                dma((CHUNKS,)),
                dma((3,)),
                dma((2, peers, CHUNKS)),
                dma((2, peers, CHUNKS)),
                dma((2, CHUNKS)),
                dma((2, CHUNKS)),
                dma((2,)),
                dma((2,)),
                dma((2,)),
                dma((2, 2)),
                dma((2, 2)),
                dma((2, 2, peers)),
                dma((2, 2, peers)),
                dma((2, 2)),
                dma((2, 2)),
                pltpu.SemaphoreType.REGULAR,
                dma((2, tiles)),
                dma((tiles,)),
                dma((tiles,)),
                dma((2, tiles)),
                dma((tiles,)),
                dma((tiles,)),
            ],
            compiler_params=pltpu.CompilerParams(
                collective_id=0, has_side_effects=True, vmem_limit_bytes=60 * 1024 * 1024
            ),
        )(text, gain.reshape(1, depth), image, wq, wk, wv, wo, selected)

    in_specs = (
        P("seq", None),
        P(),
        P("seq", None),
        P(None, ("section", "head")),
        P(None, ("section", "head")),
        P(None, ("section", "head")),
        P(("section", "head"), None),
        P("seq", None),
    )
    out_specs = P("seq", ("section", "head"))
    return jax.shard_map(shards, mesh=mesh, in_specs=in_specs, out_specs=out_specs, check_vma=False)
```

profile of v0, /device:TPU:1, one launch (start us, length us, event | category | flops | bytes accessed | tf_op | source)
XLA Modules:
  0.0 104.9 jit_solution(3780054782077751465)
XLA Ops:
  0.0 102.6 %shard_map.82 = bf16[1024,512]{1,0:T(8,128)(2,1)} custom-call(bf16[1024,4096]{1,0:T(8,128)(2,1)} %text_hbm.1, f32[1,4096]{1,0:T(1,128)} %bitcast.1, bf16[2048,1024]{1,0:T(8,128)(2,1)} %image_hbm.1, bf16[4096,512]{1,0:T(8,128)(2,1)} %wq_hbm.1, bf16[1024,128]{1,0:T(8,128)(2,1)} %wk_hbm.1, bf16[1024,128]{1,0:T(8,128)(2,1)} %wv_hbm.1, bf16[512,4096]{1,0:T(8,128)(2,1)} %wo_hbm.1, ...), custom_call_target="tpu_custom_call" | custom-call | tf_op jit(solution)/shard_map/pallas_call | solution.py:512
  102.6 2.3 %copy.10 = bf16[1024,512]{1,0:T(8,128)(2,1)} copy(bf16[1024,512]{1,0:T(8,128)(2,1)} %shard_map.82) | data formatting | bytes 2097152
where the time goes:
time: 105 us
  Pallas kernels  103 us (98%)
  local copies, waits for them, and re-layouts  2.26 us (2%)
    pallas_call x1, Pallas kernels, shards(): pl.pallas_call(functools.partial(kernel, (n_sec, n_seq, n_head)), out_sha...  103 us
    unnamed x1, local copies, waits for them, and re-layouts  2.26 us

commit v1 on v0

--- a/solution.py
+++ b/solution.py
@@ -12,8 +12,6 @@
 BLOCK = 64
 EPSILON = 1e-05
 CHUNKS = 4
-PART_LAG = 4
-OUT_LAG = 2
 MESH = pl.DeviceIdType.MESH
 
 
@@ -64,6 +62,8 @@
     r_core,
     p_send,
     p_recv,
+    f_send,
+    f_recv,
 ):
     n_sec, n_seq, n_head = sizes
     sec = lax.axis_index("section")
@@ -89,6 +89,8 @@
     far = sec + 1 - 2 * lax.rem(sec, 2)
     buddy_far = buddy + 1 - 2 * lax.rem(buddy, 2)
     first = head == 0
+    mine, theirs = jnp.where(first, far, sec), jnp.where(first, sec, far)
+    mine_there, theirs_there = jnp.where(first, buddy_far, buddy), jnp.where(first, buddy, buddy_far)
 
     def at(s, h):
         return {"section": s, "seq": seq, "head": h}
@@ -125,9 +127,6 @@
     weight_loads[0].start()
     weight_loads[1].start()
     for load in image_loads:
-        load.start()
-    weight_loads[2].start()
-    for load in text_loads:
         load.start()
 
     barrier = pltpu.get_barrier_semaphore()
@@ -152,19 +151,19 @@
 
     wo_own = [
         pltpu.make_async_copy(
-            wo_hbm.at[:, wo_cols((sec, far)[side], head)], wo_all.at[side, slot(0, head)], wo_local.at[side]
+            wo_hbm.at[:, wo_cols(mine, side)], wo_all.at[side, slot(0, head)], wo_local.at[side]
         )
         for side in range(2)
     ]
     wo_near = [
         remote(
-            wo_hbm.at[:, wo_cols((sec, far)[side], other)],
+            wo_hbm.at[:, wo_cols(theirs, side)],
             wo_all.at[side, slot(0, head)],
             wo_send.at[side],
             wo_recv.at[side],
             at(sec, other),
         )
-        for side in (1, 0)
+        for side in range(2)
     ]
     piece_rows = wo_hbm.shape[0] // n_seq
 
@@ -174,18 +173,27 @@
     wo_far = [
         remote(
             wo_hbm.at[
-                pl.ds(pl.multiple_of(seq * piece_rows, piece_rows), piece_rows), wo_cols((buddy, buddy_far)[side], h)
+                pl.ds(pl.multiple_of(seq * piece_rows, piece_rows), piece_rows), wo_cols((mine_there, theirs_there)[i], side)
             ],
             piece_at(side, head, seq),
             z_send.at[side, i],
             z_recv.at[side, i],
             at(buddy, h),
         )
-        for side in (1, 0)
         for i, h in enumerate((head, other))
+        for side in range(2)
     ]
-    for copy in wo_far + wo_own + wo_near:
-        copy.start()
+    wo_first, wo_second = wo_far[:2], wo_far[2:]
+
+    @pl.when(first)
+    def _():
+        for copy in wo_first:
+            copy.start()
+
+    @pl.when(jnp.logical_not(first))
+    def _():
+        for copy in wo_second:
+            copy.start()
 
     weight_loads[0].wait()
     weight_loads[1].wait()
@@ -229,6 +237,10 @@
 
     for c in range(CHUNKS):
         image_loads[c].wait()
+        if c == CHUNKS // 2:
+            weight_loads[2].start()
+            for load in text_loads:
+                load.start()
         both = jnp.dot(
             image[c * chunk_rows : (c + 1) * chunk_rows, :], wkv[...], preferred_element_type=jnp.float32
         ).astype(jnp.bfloat16)
@@ -243,6 +255,9 @@
     @pl.when(first)
     def _():
         kv_start_late()
+
+    for copy in wo_own + wo_near:
+        copy.start()
 
     weight_loads[2].wait()
     for load in text_loads:
@@ -262,6 +277,20 @@
         return carry
 
     lax.fori_loop(0, text_step, query_step, 0)
+
+    @pl.when(first)
+    def _():
+        for copy in wo_first:
+            copy.wait_send()
+        for copy in wo_second:
+            copy.start()
+
+    @pl.when(jnp.logical_not(first))
+    def _():
+        for copy in wo_second:
+            copy.wait_send()
+        for copy in wo_first:
+            copy.start()
 
     def kv_arrival(kind, peer_at, c):
         ref = (k_all, v_all)[kind]
@@ -355,11 +384,6 @@
             kv_arrival(1, 0, c).wait_recv()
             kv_forward(1, c).start()
 
-    @pl.when(jnp.logical_not(first))
-    def _():
-        spread_wo(1)
-        spread_wo(0)
-
     for c in range(CHUNKS - 1):
         kv_done(c)
 
@@ -368,6 +392,11 @@
         pl.semaphore_signal(go_sem, inc=1, device_id=at(sec, other), device_id_type=MESH)
 
     kv_done(CHUNKS - 1)
+
+    @pl.when(first)
+    def _():
+        for side in range(2):
+            spread_wo(side)
 
     def own_copies(t):
         tile = att.at[slot(0, head), t]
@@ -380,8 +409,13 @@
         tile = att.at[slot(1, head), t]
         return remote(tile, tile, a_core.at[t], r_core.at[1, t], at(sec, other))
 
-    def part_copy(t):
-        return remote(part_out.at[t], part_in.at[t], p_send.at[t], p_recv.at[t], at(far, head))
+    def part_copy(side, t):
+        return remote(
+            part_out.at[side, t], part_in.at[side, t], p_send.at[side, t], p_recv.at[side, t], at(far, other)
+        )
+
+    def final_copy(t):
+        return remote(part_out.at[0, t], part_in.at[0, t], f_send.at[t], f_recv.at[t], at(sec, other))
 
     def attend(t):
         for j in range(topk):
@@ -409,10 +443,9 @@
             total = term if total is None else total + term
         return total
 
-    lag_part = jnp.where(first, tiles + 1, PART_LAG)
-    lag_out = jnp.where(first, tiles + 1 + OUT_LAG, tiles + OUT_LAG)
-    at_spread = tiles - 1
-    at_forward = jnp.where(first, tiles, PART_LAG - 1)
+    second = jnp.logical_not(first)
+    at_forward = tiles // 2
+    lag = jnp.where(first, tiles + 1, tiles)
 
     def step(s, carry):
         @pl.when(s < tiles)
@@ -428,47 +461,71 @@
             remote(there, there, a_send.at[0, t], r_pair.at[t], at(buddy, head)).wait_recv()
             pair_forward(t).start()
 
-        @pl.when(first & (s == at_spread))
-        def _():
-            spread_wo(1)
-            spread_wo(0)
+        @pl.when(second & (s == 1))
+        def _():
+            for side in range(2):
+                spread_wo(side)
 
         @pl.when(s == at_forward)
         def _():
-            forward_wo(1)
-
-        @pl.when(s == at_forward + 1)
-        def _():
-            wo_arrived(1)
-            forward_wo(0)
-
-        @pl.when((s >= lag_part) & (s < tiles + lag_part))
-        def _():
-            t = s - lag_part
+            for side in range(2):
+                forward_wo(side)
+
+        @pl.when(s == lag)
+        def _():
+            for side in range(2):
+                wo_arrived(side)
+
+        @pl.when((s >= lag) & (s < tiles + lag))
+        def _():
+            t = s - lag
+            rows = pl.ds(pl.multiple_of(t * TILE, TILE), TILE)
             for flag in range(2):
                 there = att.at[slot(flag, other), t]
                 remote(there, there, a_send.at[1, t], r_core.at[flag, t], at(sec, other)).wait_recv()
-            part_out[t] = product(1, t).astype(jnp.bfloat16)
-            part_copy(t).start()
-
-        @pl.when(s == lag_out)
-        def _():
-            wo_arrived(0)
-
-        @pl.when((s >= lag_out) & (s < tiles + lag_out))
-        def _():
-            t = s - lag_out
-            own = product(0, t)
-            part_copy(t).wait_recv()
-            out_ref[pl.ds(pl.multiple_of(t * TILE, TILE), TILE), :] = (own + part_in[t].astype(jnp.float32)).astype(
-                out_ref.dtype
-            )
+
+            @pl.when(first)
+            def _():
+                for side in range(2):
+                    part_out[side, t] = product(side, t).astype(jnp.bfloat16)
+                    part_copy(side, t).start()
+
+            @pl.when(second)
+            def _():
+                for side in range(2):
+                    own = product(side, t)
+                    part_copy(side, t).wait_recv()
+                    total = (own + part_in[side, t].astype(jnp.float32)).astype(jnp.bfloat16)
+                    if side == 0:
+                        part_out[0, t] = total
+                        final_copy(t).start()
+                    else:
+                        out_ref[rows, :] = total
 
         return carry
 
-    lax.fori_loop(0, 2 * tiles + 1 + OUT_LAG, step, 0)
-
-    for copy in wo_near + wo_far:
+    lax.fori_loop(0, 2 * tiles + 1, step, 0)
+
+    def take(t, carry):
+        final_copy(t).wait_recv()
+        out_ref[pl.ds(pl.multiple_of(t * TILE, TILE), TILE), :] = part_in[0, t]
+        return carry
+
+    @pl.when(first)
+    def _():
+        lax.fori_loop(0, tiles, take, 0)
+
+    @pl.when(first)
+    def _():
+        for copy in wo_second:
+            copy.wait_send()
+
+    @pl.when(second)
+    def _():
+        for copy in wo_first:
+            copy.wait_send()
+
+    for copy in wo_near:
         copy.wait_send()
     for side in range(2):
         for i in range(2):
@@ -484,8 +541,18 @@
                 kv_forward(kind, c).wait_send()
 
     def drain(t, carry):
-        for copy in own_copies(t) + (pair_forward(t), part_copy(t)):
+        for copy in own_copies(t) + (pair_forward(t),):
             copy.wait_send()
+
+        @pl.when(first)
+        def _():
+            for side in range(2):
+                part_copy(side, t).wait_send()
+
+        @pl.when(second)
+        def _():
+            final_copy(t).wait_send()
+
         return carry
 
     lax.fori_loop(0, tiles, drain, 0)
@@ -520,8 +587,8 @@
                 pltpu.VMEM(wq.shape, bf16),
                 pltpu.VMEM((wk.shape[0], 2 * width), bf16),
                 pltpu.VMEM((2, 2 * n_head, wo.shape[0], out_cols), bf16),
-                pltpu.VMEM((tiles, TILE, out_cols), bf16),
-                pltpu.VMEM((tiles, TILE, out_cols), bf16),
+                pltpu.VMEM((2, tiles, TILE, out_cols), bf16),
+                pltpu.VMEM((2, tiles, TILE, out_cols), bf16),
                 pltpu.VMEM((blocks, BLOCK, width), bf16),
                 pltpu.VMEM((blocks, BLOCK, width), bf16),
                 pltpu.VMEM((tiles, cols_q // HEAD_DIM * TILE, HEAD_DIM), bf16),
@@ -549,6 +616,8 @@
                 dma((tiles,)),
                 dma((tiles,)),
                 dma((2, tiles)),
+                dma((2, tiles)),
+                dma((2, tiles)),
                 dma((tiles,)),
                 dma((tiles,)),
             ],

time: 105 us -> 101 us (0.962)
  Pallas kernels: 103 us -> 98.6 us
    pallas_call x1, Pallas kernels: 103 us -> 98.6 us  [shards(): pl.pallas_call(functools.partial(kernel, (n_sec, n_seq, n_head)), out_sha...]
where the time goes in v1:
time: 101 us
  Pallas kernels  98.6 us (98%)
  local copies, waits for them, and re-layouts  2.26 us (2%)
    pallas_call x1, Pallas kernels, shards(): pl.pallas_call(functools.partial(kernel, (n_sec, n_seq, n_head)), out_sha...  98.6 us
    unnamed x1, local copies, waits for them, and re-layouts  2.26 us

profile of v1, /device:TPU:1, one launch (start us, length us, event | category | flops | bytes accessed | tf_op | source)
XLA Modules:
  0.0 100.9 jit_solution(9922751804951967710)
XLA Ops:
  0.0 98.6 %shard_map.82 = bf16[1024,512]{1,0:T(8,128)(2,1)} custom-call(bf16[1024,4096]{1,0:T(8,128)(2,1)} %text_hbm.1, f32[1,4096]{1,0:T(1,128)} %bitcast.1, bf16[2048,1024]{1,0:T(8,128)(2,1)} %image_hbm.1, bf16[4096,512]{1,0:T(8,128)(2,1)} %wq_hbm.1, bf16[1024,128]{1,0:T(8,128)(2,1)} %wk_hbm.1, bf16[1024,128]{1,0:T(8,128)(2,1)} %wv_hbm.1, bf16[512,4096]{1,0:T(8,128)(2,1)} %wo_hbm.1, ...), custom_call_target="tpu_custom_call" | custom-call | tf_op jit(solution)/shard_map/pallas_call | solution.py:579
  98.6 2.3 %copy.10 = bf16[1024,512]{1,0:T(8,128)(2,1)} copy(bf16[1024,512]{1,0:T(8,128)(2,1)} %shard_map.82) | data formatting | bytes 2097152

commit v2 on v1

--- a/solution.py
+++ b/solution.py
@@ -263,6 +263,29 @@
     for load in text_loads:
         load.wait()
 
+    def kv_arrival(kind, peer_at, c):
+        ref = (k_all, v_all)[kind]
+        back = peer_at if ring else len(peers) - 1 - peer_at
+        there = chunk_at(ref, peers[back], c)
+        return remote(there, there, kv_send.at[kind, peer_at, c], kv_recv.at[kind, peer_at, c], at_seq(peers[peer_at]))
+
+    def kv_forward(kind, c):
+        ref = (k_all, v_all)[kind]
+        came, goes = ((across, beside), (beside, across))[kind]
+        there = chunk_at(ref, came, c)
+        return remote(there, there, fwd_send.at[kind, c], fwd_recv.at[kind, c], at_seq(goes))
+
+    def kv_forwarded(kind, c):
+        ref = (k_all, v_all)[kind]
+        there = chunk_at(ref, 3 - seq, c)
+        return remote(there, there, fwd_send.at[kind, c], fwd_recv.at[kind, c], at_seq(seq))
+
+    def forward_kv(c):
+        kv_arrival(0, 1, c).wait_recv()
+        kv_forward(0, c).start()
+        kv_arrival(1, 0, c).wait_recv()
+        kv_forward(1, c).start()
+
     def query_step(i, carry):
         part = pl.ds(pl.multiple_of(i * text_rows, text_rows), text_rows)
         as_float = text[part, :].astype(jnp.float32)
@@ -274,6 +297,13 @@
                 q_all[i * (text_rows // TILE) + u, h * TILE : (h + 1) * TILE, :] = queries[
                     u * TILE : (u + 1) * TILE, h * HEAD_DIM : (h + 1) * HEAD_DIM
                 ]
+        if ring:
+            for c in range(CHUNKS):
+
+                @pl.when(first & (i == min(c, text_step - 1)))
+                def _():
+                    forward_kv(c)
+
         return carry
 
     lax.fori_loop(0, text_step, query_step, 0)
@@ -291,23 +321,6 @@
             copy.wait_send()
         for copy in wo_first:
             copy.start()
-
-    def kv_arrival(kind, peer_at, c):
-        ref = (k_all, v_all)[kind]
-        back = peer_at if ring else len(peers) - 1 - peer_at
-        there = chunk_at(ref, peers[back], c)
-        return remote(there, there, kv_send.at[kind, peer_at, c], kv_recv.at[kind, peer_at, c], at_seq(peers[peer_at]))
-
-    def kv_forward(kind, c):
-        ref = (k_all, v_all)[kind]
-        came, goes = ((across, beside), (beside, across))[kind]
-        there = chunk_at(ref, came, c)
-        return remote(there, there, fwd_send.at[kind, c], fwd_recv.at[kind, c], at_seq(goes))
-
-    def kv_forwarded(kind, c):
-        ref = (k_all, v_all)[kind]
-        there = chunk_at(ref, 3 - seq, c)
-        return remote(there, there, fwd_send.at[kind, c], fwd_recv.at[kind, c], at_seq(seq))
 
     @pl.when(jnp.logical_not(first))
     def _():
@@ -377,12 +390,11 @@
                 for p in range(len(peers)):
                     g_arrival(side, i, p).wait_recv()
 
-    if ring:
-        for c in range(CHUNKS):
-            kv_arrival(0, 1, c).wait_recv()
-            kv_forward(0, c).start()
-            kv_arrival(1, 0, c).wait_recv()
-            kv_forward(1, c).start()
+    @pl.when(jnp.logical_not(first))
+    def _():
+        if ring:
+            for c in range(CHUNKS):
+                forward_kv(c)
 
     for c in range(CHUNKS - 1):
         kv_done(c)
@@ -392,11 +404,6 @@
         pl.semaphore_signal(go_sem, inc=1, device_id=at(sec, other), device_id_type=MESH)
 
     kv_done(CHUNKS - 1)
-
-    @pl.when(first)
-    def _():
-        for side in range(2):
-            spread_wo(side)
 
     def own_copies(t):
         tile = att.at[slot(0, head), t]
@@ -444,7 +451,8 @@
         return total
 
     second = jnp.logical_not(first)
-    at_forward = tiles // 2
+    at_spread = jnp.where(first, tiles // 4, 1)
+    at_forward = jnp.where(first, 3 * tiles // 4, 3 * tiles // 8)
     lag = jnp.where(first, tiles + 1, tiles)
 
     def step(s, carry):
@@ -461,7 +469,7 @@
             remote(there, there, a_send.at[0, t], r_pair.at[t], at(buddy, head)).wait_recv()
             pair_forward(t).start()
 
-        @pl.when(second & (s == 1))
+        @pl.when(s == at_spread)
         def _():
             for side in range(2):
                 spread_wo(side)

time: 101 us -> 100 us (0.990)
  no operation moved by 1% of the time
where the time goes in v2:
time: 100 us
  Pallas kernels  97.7 us (98%)
  local copies, waits for them, and re-layouts  2.26 us (2%)
    pallas_call x1, Pallas kernels, shards(): pl.pallas_call(functools.partial(kernel, (n_sec, n_seq, n_head)), out_sha...  97.7 us
    unnamed x1, local copies, waits for them, and re-layouts  2.26 us

profile of v2, /device:TPU:1, one launch (start us, length us, event | category | flops | bytes accessed | tf_op | source)
XLA Modules:
  0.0 100.0 jit_solution(12258975253529769932)
XLA Ops:
  0.0 97.7 %shard_map.82 = bf16[1024,512]{1,0:T(8,128)(2,1)} custom-call(bf16[1024,4096]{1,0:T(8,128)(2,1)} %text_hbm.1, f32[1,4096]{1,0:T(1,128)} %bitcast.1, bf16[2048,1024]{1,0:T(8,128)(2,1)} %image_hbm.1, bf16[4096,512]{1,0:T(8,128)(2,1)} %wq_hbm.1, bf16[1024,128]{1,0:T(8,128)(2,1)} %wk_hbm.1, bf16[1024,128]{1,0:T(8,128)(2,1)} %wv_hbm.1, bf16[512,4096]{1,0:T(8,128)(2,1)} %wo_hbm.1, ...), custom_call_target="tpu_custom_call" | custom-call | tf_op jit(solution)/shard_map/pallas_call | solution.py:587
  97.7 2.3 %copy.10 = bf16[1024,512]{1,0:T(8,128)(2,1)} copy(bf16[1024,512]{1,0:T(8,128)(2,1)} %shard_map.82) | data formatting | bytes 2097152
